TPU v7x, 32 devices: a whole 2x2x4 slice. The times are simulated.
32 devices in a mesh: clip: 4 (over y, core), seq: 8 (over z, x).
Axes of the slice: x: 2, y: 2, z: 4, core: 2. Of those that a mesh axis runs over, the one named last changes fastest.
Arguments:
- block_input: bfloat16 [64, 384, 1152], P('clip', 'seq'), parts along dimension 0, may hold values from -160 to 160
- mid_state: bfloat16 [64, 384, 1152], P('clip', 'seq'), parts along dimension 0, may hold values from -160 to 160
- saved_qkv: bfloat16 [3, 64, 384, 576], P(None, 'clip', 'seq'), parts along dimension 1, may hold values from -6 to 6
- out_grad: bfloat16 [64, 384, 1152], P('clip', 'seq'), parts along dimension 0, may hold values from -6 to 6
- modulation: float32 [20, 1152], P('clip'), parts along dimension 0, may hold values from -3 to 3
- w_qkv_s: bfloat16 [1152, 1728], replicated, may hold values from -0.1875 to 0.1875
- w_out_s: bfloat16 [576, 1152], replicated, may hold values from -0.25 to 0.25
- w_qkv_t: bfloat16 [1152, 1728], replicated, may hold values from -0.1875 to 0.1875
- w_out_t: bfloat16 [576, 1152], replicated, may hold values from -0.25 to 0.25
- qk_gain: float32 [4, 72], replicated, may hold values from 0.1 to 1.9
Outputs:
- input_grad: bfloat16 [64, 384, 1152], P('clip', 'seq'), parts along dimension 0
- mod_grad: float32 [24, 1152], P('clip'), parts along dimension 0
There are 4 independent parts, one for each index of `clip`. A program takes and returns all parts, laid end to end along the dimension named above; an argument that names none is the same for every part. Nothing has to cross between parts.
All inputs are finite; a program needn't handle non-finite values.
Results may differ from a plain program's by a relative error of at most 0.0057.
Values may be sent and summed in bfloat16 or wider, within the bound.
No kernel may reach another device: no remote copies, remote signals or barrier semaphores. Data moves between devices by JAX's collectives and lax.ppermute only.
A program may use at most 128 MiB of HBM per device.

v0:
```python
import jax
import jax.numpy as jnp
from jax import lax
from jax.sharding import PartitionSpec as P

HEADS = 8
HEAD_DIM = 72
WIDTH = 576
NORM_EPS = 1e-06


def layer_stats(inputs):
    values = inputs.astype(jnp.float32)
    centre = jnp.mean(values, axis=-1, keepdims=True)
    spread = jnp.mean(jnp.square(values - centre), axis=-1, keepdims=True)
    inverse = lax.rsqrt(spread + NORM_EPS)
    return ((values - centre) * inverse, inverse)


def modulate(normed, offset, stretch):
    return (normed * (1.0 + stretch) + offset).astype(jnp.bfloat16)


def matmul_rows(left_rows, weight):
    flattened = left_rows.reshape(-1, left_rows.shape[-1])
    result = jnp.dot(flattened, weight, preferred_element_type=jnp.float32)
    return result.reshape(left_rows.shape[:-1] + (weight.shape[1],))


def matmul_back(left_rows, weight):
    flattened = left_rows.reshape(-1, left_rows.shape[-1])
    result = lax.dot_general(
        flattened, weight, (((1,), (1,)), ((), ())), preferred_element_type=jnp.float32
    )
    return result.reshape(left_rows.shape[:-1] + (weight.shape[0],))


def head_split(tensor):
    return tensor.reshape(tensor.shape[:-1] + (HEADS, HEAD_DIM))


def rms_normed(raw_rows, gain_row):
    values = head_split(raw_rows).astype(jnp.float32)
    inverse = lax.rsqrt(jnp.mean(values * values, axis=-1, keepdims=True) + NORM_EPS)
    return ((values * inverse * gain_row).astype(jnp.bfloat16), values, inverse)


def rms_back(values, inverse, gain_row, upstream):
    scaled = gain_row * upstream
    result = inverse * scaled - values * (inverse * inverse * inverse) * jnp.mean(
        values * scaled, axis=-1, keepdims=True
    )
    return result.astype(jnp.bfloat16).reshape(values.shape[:-2] + (-1,))


def attend(queries, key_rows, value_rows, out_cot, query_gain, key_gain):
    query_norm, query_raw, query_inv = rms_normed(queries, query_gain)
    key_norm, key_raw, key_inv = rms_normed(key_rows, key_gain)
    factor = HEAD_DIM ** (-0.5)
    scores = (
        jnp.einsum("blhd,bmhd->bhlm", query_norm, key_norm, preferred_element_type=jnp.float32)
        * factor
    )
    exp_scores = jnp.exp(scores)
    attn_probs = exp_scores / jnp.sum(exp_scores, axis=-1, keepdims=True)
    probs_half = attn_probs.astype(jnp.bfloat16)
    value_heads = head_split(value_rows)
    cot_heads = head_split(out_cot)
    outputs = jnp.einsum(
        "bhlm,bmhd->blhd", probs_half, value_heads, preferred_element_type=jnp.float32
    ).astype(jnp.bfloat16)
    prob_grad = jnp.einsum(
        "blhd,bmhd->bhlm", cot_heads, value_heads, preferred_element_type=jnp.float32
    )
    row_inner = jnp.sum(attn_probs * prob_grad, axis=-1, keepdims=True)
    score_grad = (attn_probs * (prob_grad - row_inner) * factor).astype(jnp.bfloat16)
    value_grad = jnp.einsum(
        "bhlm,blhd->bmhd", probs_half, cot_heads, preferred_element_type=jnp.float32
    ).astype(jnp.bfloat16)
    qnorm_grad = jnp.einsum(
        "bhlm,bmhd->blhd", score_grad, key_norm, preferred_element_type=jnp.float32
    )
    knorm_grad = jnp.einsum(
        "bhlm,blhd->bmhd", score_grad, query_norm, preferred_element_type=jnp.float32
    )
    merged = outputs.shape[:-2] + (-1,)
    return (
        outputs.reshape(merged),
        rms_back(query_raw, query_inv, query_gain, qnorm_grad),
        rms_back(key_raw, key_inv, key_gain, knorm_grad),
        value_grad.reshape(merged),
    )


def output_cot(cotangent, gate_row, w_out):
    scaled = (cotangent.astype(jnp.float32) * gate_row).astype(jnp.bfloat16)
    return matmul_back(scaled, w_out).astype(jnp.bfloat16)


def gate_term(cotangent, outputs, w_out):
    branch = matmul_rows(outputs, w_out)
    return jnp.sum((cotangent.astype(jnp.float32) * branch).reshape(-1, branch.shape[-1]), axis=0)


def input_branch(grad_parts, w_qkv, normed, inverse, stretch):
    joined = jnp.concatenate(grad_parts, axis=-1)
    mod_cot = matmul_back(joined, w_qkv)
    columns = mod_cot.shape[-1]
    offset_term = jnp.sum(mod_cot.reshape(-1, columns), axis=0)
    stretch_term = jnp.sum((mod_cot * normed).reshape(-1, columns), axis=0)
    norm_cot = mod_cot * (1.0 + stretch)
    branch = inverse * (
        norm_cot
        - jnp.mean(norm_cot, axis=-1, keepdims=True)
        - normed * jnp.mean(norm_cot * normed, axis=-1, keepdims=True)
    )
    return (branch, offset_term, stretch_term)


def swapped(tensor):
    return jnp.swapaxes(tensor, 0, 1)


def body(
    block_input,
    mid_state,
    saved_qkv,
    out_grad,
    modulation,
    w_qkv_s,
    w_out_s,
    w_qkv_t,
    w_out_t,
    qk_gain,
):
    normed_mid, inverse_mid = layer_stats(mid_state)
    temporal_cot = output_cot(out_grad, modulation[4], w_out_t)
    temporal_res = attend(
        swapped(saved_qkv[0]),
        swapped(saved_qkv[1]),
        swapped(saved_qkv[2]),
        swapped(temporal_cot),
        qk_gain[2],
        qk_gain[3],
    )
    temporal_gate = gate_term(out_grad, swapped(temporal_res[0]), w_out_t)
    temporal_branch, temporal_offset, temporal_stretch = input_branch(
        tuple((swapped(grad_piece) for grad_piece in temporal_res[1:])),
        w_qkv_t,
        normed_mid,
        inverse_mid,
        modulation[3],
    )
    mid_grad = (out_grad.astype(jnp.float32) + temporal_branch).astype(jnp.bfloat16)
    arrived, landed = (
        lax.all_to_all(block_input, "seq", split_axis=0, concat_axis=1, tiled=True),
        lax.all_to_all(mid_grad, "seq", split_axis=0, concat_axis=1, tiled=True),
    )
    normed_fr, inverse_fr = layer_stats(arrived)
    frame_mod = modulate(normed_fr, modulation[0], modulation[1])
    frame_qkv = matmul_rows(frame_mod, w_qkv_s).astype(jnp.bfloat16)
    frame_cot = output_cot(landed, modulation[2], w_out_s)
    frame_res = attend(
        frame_qkv[..., :WIDTH],
        frame_qkv[..., WIDTH : 2 * WIDTH],
        frame_qkv[..., 2 * WIDTH :],
        frame_cot,
        qk_gain[0],
        qk_gain[1],
    )
    spatial_gate = gate_term(landed, frame_res[0], w_out_s)
    frame_branch, spatial_offset, spatial_stretch = input_branch(
        frame_res[1:], w_qkv_s, normed_fr, inverse_fr, modulation[1]
    )
    outgoing = frame_branch.astype(jnp.bfloat16)
    returned = lax.all_to_all(outgoing, "seq", split_axis=1, concat_axis=0, tiled=True)
    term_stack = jnp.stack(
        [
            spatial_offset,
            spatial_stretch,
            spatial_gate,
            temporal_offset,
            temporal_stretch,
            temporal_gate,
        ]
    )
    totals = lax.psum(term_stack, "seq")
    token_count = block_input.shape[0] * block_input.shape[1] * lax.axis_size("seq")
    mod_grad = totals * token_count ** (-0.5)
    input_grad = (mid_grad.astype(jnp.float32) + returned.astype(jnp.float32)).astype(jnp.bfloat16)
    return (input_grad, mod_grad)


def solution(mesh):
    return jax.shard_map(
        body,
        mesh=mesh,
        in_specs=(
            P("clip", "seq", None),
            P("clip", "seq", None),
            P(None, "clip", "seq", None),
            P("clip", "seq", None),
            P("clip", None),
            P(),
            P(),
            P(),
            P(),
            P(),
        ),
        out_specs=(P("clip", "seq", None), P("clip", None)),
        check_vma=False,
    )
```

profile of v0, /device:TPU:0, one launch (start us, length us, event | category | flops | bytes accessed | tf_op | source)
XLA Modules:
  0.0 314.7 jit_solution(16981990342659741506)
XLA Ops:
  0.7 7.6 %all-to-all-start = ((bf16[16,48,1152]{2,1,0:T(8,128)(2,1)}), bf16[16,48,1152]{2,1,0:T(8,128)(2,1)}, u32[]{:S(2)}, u32[]{:S(2)}) async-start(bf16[16,48,1152]{2,1,0:T(8,128)(2,1)} %param.10), calls=%async_computation | async-start | bytes 3538944 | tf_op jit(solution)/shard_map/all_to_all | solution.py:156
  9.5 2.6 fusion.98
  12.2 3.8 %reshape.326 = bf16[48,16,8,72]{3,2,0,1:T(8,128)(2,1)} reshape(bf16[48,16,576]{2,0,1:T(8,128)(2,1)} %fusion.98) | data formatting | bytes 1769472 | tf_op jit(solution)/shard_map/reshape | solution.py:39
  16.0 3.8 %convert_bitcast_fusion.1 = (f32[48,16,576]{2,0,1:T(8,128)S(1)}, bf16[48,16,576]{2,0,1:T(8,128)(2,1)}, f32[48,16,576]{2,0,1:T(8,128)}) fusion(bf16[3,16,48,576]{3,2,1,0:T(8,128)(2,1)} %param.12), kind=kLoop, calls=%fused_computation.88 | loop fusion | flops 884736 | bytes 7077888 | tf_op jit(solution)/shard_map/convert_element_type | solution.py:43
  23.0 2.9 multiply_reduce_fusion.7
  31.6 2.8 reshape.338
  34.4 2.9 multiply_reduce_fusion.6
  38.3 5.2 %fusion.94 = f32[48,8,16,16]{2,3,1,0:T(8,128)} fusion(bf16[48,16,8,72]{3,2,0,1:T(8,128)(2,1)S(1)} %copy-done.11, bf16[48,16,8,72]{3,2,0,1:T(8,128)(2,1)} %reshape.326), kind=kOutput, calls=%fused_computation.120 | convolution fusion | flops 14155776 | bytes 2162688 | tf_op jit(solution)/shard_map/blhd,bmhd->bhlm/dot_general | solution.py:72
  49.8 11.1 %fusion.38 = (f32[48,16,8]{1,2,0:T(8,128)}, f32[48,8,72,16]{2,3,1,0:T(8,128)}) fusion(f32[48,16,8,72]{3,2,1,0:T(8,128)} %reshape.338, f32[72]{0:T(128)S(1)} %copy-done.35, f32[48,8,16,16]{2,3,1,0:T(8,128)} %fusion.94, f32[48,8,16]{2,1,0:T(8,128)S(1)} %get-tuple-element.33, f32[48,8,16,16]{2,3,1,0:T(8,128)} %copy-done.19, f32[48,16,8,72]{3,2,1,0:T(8,128)} %reshape.337, ...), kind=kOutput, calls=%fused_computation.53 | convolution fusion | flops 17694736 | bytes 6169152 | tf_op jit(solution)/shard_map/bhlm,blhd->bmhd/dot_general | solution.py:83
  60.9 12.1 %fusion.41 = (f32[48,16,8]{1,2,0:T(8,128)}, f32[48,8,72,16]{2,3,1,0:T(8,128)}) fusion(f32[48,16,8,72]{3,2,1,0:T(8,128)} %reshape.337, f32[72]{0:T(128)S(1)} %copy-done.36, f32[48,8,16,16]{2,3,1,0:T(8,128)} %fusion.94, f32[48,8,16]{2,1,0:T(8,128)S(1)} %get-tuple-element.33, f32[48,8,16,16]{2,3,1,0:T(8,128)} %copy-done.19, f32[48,16,8,72]{3,2,1,0:T(8,128)} %reshape.338, ...), kind=kOutput, calls=%fused_computation.58 | convolution fusion | flops 17694736 | bytes 6169152 | tf_op jit(solution)/shard_map/bhlm,bmhd->blhd/dot_general | solution.py:80
  81.9 7.4 %fusion.37 = (bf16[48,16,8,72]{3,1,2,0:T(8,128)(2,1)S(1)}, bf16[48,16,8,72]{3,1,2,0:T(8,128)(2,1)S(1)}) fusion(f32[48,8,72,16]{2,3,1,0:T(8,128)} %get-tuple-element.38, f32[48,16,8,72]{3,2,1,0:T(8,128)} %reshape.338, f32[48,16,8]{1,2,0:T(8,128)} %copy.208, f32[48,16,8]{1,2,0:T(8,128)} %copy.204, f32[72]{0:T(128)S(1)} %copy-done.35, ...), kind=kLoop, calls=%fused_computation.52 | loop fusion | flops 5308416 | bytes 8995392 | tf_op jit(solution)/shard_map/convert_element_type | solution.py:53
  90.9 3.6 %reshape.329 = bf16[48,16,576]{2,1,0:T(8,128)(2,1)} reshape(bf16[48,16,8,72]{3,2,1,0:T(8,128)(2,1)} %copy.209) | data formatting | bytes 1769472 | tf_op jit(solution)/shard_map/reshape | solution.py:53
  96.1 3.8 %reshape.328 = bf16[48,16,576]{2,1,0:T(8,128)(2,1)} reshape(bf16[48,16,8,72]{3,2,1,0:T(8,128)(2,1)} %copy.203) | data formatting | bytes 1769472 | tf_op jit(solution)/shard_map/reshape | solution.py:53
  99.9 5.0 %concatenate.13 = bf16[16,48,1728]{2,0,1:T(8,128)(2,1)} concatenate(bf16[16,48,576]{2,0,1:T(8,128)(2,1)} %bitcast.185, bf16[16,48,576]{2,0,1:T(8,128)(2,1)S(1)} %bitcast.184, bf16[16,48,576]{2,0,1:T(8,128)(2,1)S(1)} %bitcast.183), dimensions={2} | concatenate | bytes 5308416 | tf_op jit(solution)/shard_map/concatenate | solution.py:106
  104.9 2.7 copy.212
  107.8 5.5 %fusion.138 = (f32[1152]{0:T(1024)S(1)}, f32[768]{0:T(1024)S(1)}, f32[768,1152]{1,0:T(8,128)}) fusion(f32[1152]{0:T(1024)S(1)} %copy-done.28, bf16[768,1728]{1,0:T(8,128)(2,1)S(1)} %bitcast.192, bf16[1152,1728]{0,1:T(8,128)(2,1)S(1)} %copy-done.38), kind=kOutput, calls=%fused_computation.175 | convolution fusion | flops 3060300032 | bytes 10186752 | tf_op jit(solution)/shard_map/dot_general | solution.py:32
  119.2 6.2 %all-to-all-start.1 = ((bf16[16,48,1152]{2,1,0:T(8,128)(2,1)}), bf16[16,48,1152]{2,1,0:T(8,128)(2,1)}, u32[]{:S(2)}, u32[]{:S(2)}) async-start(bf16[16,48,1152]{2,1,0:T(8,128)(2,1)} %fusion.26), calls=%async_computation.1 | async-start | bytes 3538944 | tf_op jit(solution)/shard_map/all_to_all | solution.py:157
  133.4 3.8 %fusion.33 = bf16[2,384,1728]{1,2,0:T(8,128)(2,1)S(1)} fusion(bf16[2,384,1152]{2,1,0:T(8,128)(2,1)S(1)} %add_convert_fusion, bf16[1152,1728]{0,1:T(8,128)(2,1)S(1)} %copy-done.39), kind=kOutput, calls=%fused_computation.47 | convolution fusion | flops 3058974720 | bytes 8404992 | tf_op jit(solution)/shard_map/dot_general | solution.py:26
  139.0 27.2 %all-to-all-done.1 = bf16[16,48,1152]{2,1,0:T(8,128)(2,1)} async-done(((bf16[16,48,1152]{2,1,0:T(8,128)(2,1)}), bf16[16,48,1152]{2,1,0:T(8,128)(2,1)}, u32[]{:S(2)}, u32[]{:S(2)}) %all-to-all-start.1) | async-done | bytes 1769504 | tf_op jit(solution)/shard_map/all_to_all | solution.py:157
  171.6 5.1 %fusion.148 = f32[2,8,384,384]{2,3,1,0:T(8,128)} fusion(bf16[2,384,8,72]{1,3,2,0:T(8,128)(2,1)S(1)} %bitcast.197, bf16[2,384,8,72]{1,3,2,0:T(8,128)(2,1)S(1)} %bitcast.190), kind=kOutput, calls=%fused_computation.178 | convolution fusion | flops 339738624 | bytes 11206656 | tf_op jit(solution)/shard_map/blhd,bmhd->bhlm/dot_general | solution.py:72
  178.7 3.6 %copy-done.10 = f32[2,8,384,384]{2,3,1,0:T(8,128)} copy-done((f32[2,8,384,384]{2,3,1,0:T(8,128)}, f32[2,8,384,384]{2,3,1,0:T(8,128)S(1)}, u32[]{:S(2)}) %copy-start.10) | copy-done | bytes 9437208
  182.3 3.0 fusion.105
  185.3 18.2 %fusion.63 = (f32[2,384,8]{1,2,0:T(8,128)S(1)}, f32[2,8,72,384]{3,2,1,0:T(8,128)}) fusion(bf16[2,384,8,72]{1,3,2,0:T(8,128)(2,1)S(1)} %bitcast.175, f32[72]{0:T(128)S(1)} %copy-done.33, f32[2,8,384,384]{2,3,1,0:T(8,128)} %fusion.148, f32[2,8,384]{2,1,0:T(8,128)S(1)} %get-tuple-element.40, f32[2,8,384,384]{2,3,1,0:T(8,128)} %copy-done.10, ...), kind=kOutput, calls=%fused_computation.95 | convolution fusion | flops 364511616 | bytes 22487616 | tf_op jit(solution)/shard_map/bhlm,blhd->bmhd/dot_general | solution.py:83
  203.5 17.9 %fusion.70 = (f32[2,384,8]{1,2,0:T(8,128)S(1)}, f32[2,8,72,384]{3,2,1,0:T(8,128)}) fusion(bf16[2,384,8,72]{1,3,2,0:T(8,128)(2,1)S(1)} %bitcast.181, f32[72]{0:T(128)S(1)} %copy-done.34, f32[2,8,384,384]{2,3,1,0:T(8,128)} %fusion.148, f32[2,8,384]{2,1,0:T(8,128)S(1)} %get-tuple-element.40, f32[2,8,384,384]{2,3,1,0:T(8,128)} %copy-done.10, ...), kind=kOutput, calls=%fused_computation.102 | convolution fusion | flops 364511616 | bytes 22487616 | tf_op jit(solution)/shard_map/bhlm,bmhd->blhd/dot_general | solution.py:80
  228.4 6.2 %multiply_reduce_fusion.1 = (f32[1152]{0:T(1024)S(1)}, f32[768]{0:T(1024)S(1)}, f32[768]{0:T(1024)S(1)}, f32[1152]{0:T(1024)S(1)}, f32[768,1152]{1,0:T(8,128)}) fusion(f32[8,2,48,1152]{3,2,0,1:T(8,128)S(1)} %copy-done.4, f32[768]{0:T(1024)S(1)} %rsqrt.74, f32[768]{0:T(1024)S(1)} %div.96, f32[1152]{0:T(1024)S(1)} %copy-done.29, ...), kind=kOutput, calls=%fused_computation.42 | convolution fusion | flops 3073569280 | bytes 13739520 | tf_op jit(solution)/shard_map/dot_general | solution.py:32
  234.6 3.9 %multiply_convert_fusion.1 = bf16[2,384,1152]{2,1,0:T(8,128)(2,1)S(1)} fusion(f32[2,384,1152]{2,1,0:T(8,128)} %bitcast.189, f32[8,2,48,1152]{3,2,0,1:T(8,128)} %copy-done.3, f32[2,384]{1,0:T(2,128)S(1)} %div.98, f32[2,384]{1,0:T(2,128)S(1)} %div.95, f32[1152]{0:T(1024)S(1)} %copy-done.29, f32[2,384]{1,0:T(2,128)S(1)} %div.87, f32[2,384]{1,0:T(2,128)S(1)} %rsqrt.71), kind=kLoop, calls=%fused_computation.43 | loop fusion | flops 7077888 | bytes 8864256 | tf_op jit(solution)/shard_map/convert_element_type | solution.py:175
  238.5 3.1 copy.221
  241.7 4.3 %all-to-all-start.2 = ((bf16[2,384,1152]{2,0,1:T(2,128)(2,1)}), bf16[2,384,1152]{2,0,1:T(2,128)(2,1)}, u32[]{:S(2)}, u32[]{:S(2)}) async-start(bf16[2,384,1152]{2,0,1:T(2,128)(2,1)} %copy.221), calls=%async_computation.2 | async-start | bytes 3538944 | tf_op jit(solution)/shard_map/all_to_all | solution.py:176
  246.0 3.4 %fusion.83 = bf16[48,16,8,72]{3,1,2,0:T(8,128)(2,1)S(1)} fusion(bf16[48,16,8,72]{3,2,0,1:T(8,128)(2,1)S(1)} %copy-done.12, f32[48,8,16,16]{2,3,1,0:T(8,128)} %copy-done.19, f32[48,8,16]{2,1,0:T(8,128)S(1)} %copy-done.27), kind=kOutput, calls=%fused_computation.114 | convolution fusion | flops 14893056 | bytes 2187264 | tf_op jit(solution)/shard_map/bhlm,bmhd->blhd/dot_general | solution.py:69
  251.8 3.5 %fusion.81 = f32[1152]{0:T(1024)S(1)} fusion(bf16[16,48,1152]{2,1,0:T(8,128)(2,1)} %param.13, bf16[576,1152]{1,0:T(8,128)(2,1)S(1)} %copy-done, bf16[16,48,576]{2,0,1:T(8,128)(2,1)} %bitcast.193), kind=kOutput, calls=%fused_computation.112 | convolution fusion | flops 1021868928 | bytes 3985920 | tf_op jit(solution)/shard_map/dot_general | solution.py:26
  255.3 5.6 %fusion.90 = bf16[2,8,72,384]{3,2,1,0:T(8,128)(2,1)S(1)} fusion(bf16[2,384,8,72]{1,3,2,0:T(8,128)(2,1)S(1)} %bitcast.191, f32[2,8,384,384]{2,3,1,0:T(8,128)} %copy-done.10, f32[2,8,384]{2,1,0:T(8,128)S(1)} %get-tuple-element.40), kind=kOutput, calls=%fused_computation.117 | convolution fusion | flops 347258880 | bytes 11231232 | tf_op jit(solution)/shard_map/bhlm,bmhd->blhd/dot_general | solution.py:69
  262.8 47.5 %psum.7 = f32[6,1152]{1,0:T(8,128)S(1)} all-reduce(f32[6,1152]{1,0:T(8,128)S(1)} %stack.27), channel_id=1, replica_groups=mesh['clip'=4,'seq'=8] {'seq'}, use_global_device_ids=true, to_apply=%region_26.0 | all-reduce | flops 6912 | bytes 55296 | tf_op jit(solution)/shard_map/psum | solution.py:187
  (168 shorter events, 67.4 us)
Async XLA Ops:
  0.6 8.9 %copy-start = (bf16[576,1152]{1,0:T(8,128)(2,1)S(1)}, bf16[576,1152]{1,0:T(8,128)(2,1)}, u32[]{:S(2)}) copy-start(bf16[576,1152]{1,0:T(8,128)(2,1)} %param.18) | copy-start | bytes 3981316
  0.6 7.6 %copy-start.37 = (f32[4,72]{1,0:T(4,128)S(1)}, f32[4,72]{1,0:T(4,128)}, u32[]{:S(2)}) copy-start(f32[4,72]{1,0:T(4,128)} %param.19) | copy-start | bytes 3460
  0.7 8.2 %copy-start.32 = (f32[5,1152]{1,0:T(8,128)S(1)}, f32[5,1152]{1,0:T(8,128)}, u32[]{:S(2)}) copy-start(f32[5,1152]{1,0:T(8,128)} %param.14) | copy-start | bytes 69124
  0.7 8.8 %copy-start.20 = (bf16[16,48,1152]{2,1,0:T(8,128)(2,1)S(1)}, bf16[16,48,1152]{2,1,0:T(8,128)(2,1)}, u32[]{:S(2)}) copy-start(bf16[16,48,1152]{2,1,0:T(8,128)(2,1)} %param.13) | copy-start | bytes 5308420
  0.7 118.6 %all-to-all-start = ((bf16[16,48,1152]{2,1,0:T(8,128)(2,1)}), bf16[16,48,1152]{2,1,0:T(8,128)(2,1)}, u32[]{:S(2)}, u32[]{:S(2)}) async-start(bf16[16,48,1152]{2,1,0:T(8,128)(2,1)} %param.10), calls=%async_computation | async-start | bytes 3538944 | tf_op jit(solution)/shard_map/all_to_all | solution.py:156
  23.0 3.9 %copy-start.15 = (bf16[48,16,576]{2,0,1:T(8,128)(2,1)S(1)}, bf16[48,16,576]{2,0,1:T(8,128)(2,1)}, u32[]{:S(2)}) copy-start(bf16[48,16,576]{2,0,1:T(8,128)(2,1)} %get-tuple-element.16) | copy-start | bytes 2654212
  34.4 3.9 %copy-start.11 = (bf16[48,16,8,72]{3,2,0,1:T(8,128)(2,1)S(1)}, bf16[48,16,8,72]{3,2,0,1:T(8,128)(2,1)}, u32[]{:S(2)}) copy-start(bf16[48,16,8,72]{3,2,0,1:T(8,128)(2,1)} %reshape.355) | copy-start | bytes 2654212
  38.3 5.2 %copy-start.1 = (f32[48,16,8,72]{3,2,1,0:T(8,128)S(1)}, f32[48,16,8,72]{3,2,1,0:T(8,128)}, u32[]{:S(2)}) copy-start(f32[48,16,8,72]{3,2,1,0:T(8,128)} %reshape.337) | copy-start | bytes 5308420
  38.3 5.2 %copy-start.2 = (f32[48,16,8,72]{3,2,1,0:T(8,128)S(1)}, f32[48,16,8,72]{3,2,1,0:T(8,128)}, u32[]{:S(2)}) copy-start(f32[48,16,8,72]{3,2,1,0:T(8,128)} %reshape.338) | copy-start | bytes 5308420
  38.3 5.2 %copy-start.35 = (f32[72]{0:T(128)S(1)}, f32[72]{0:T(128)}, u32[]{:S(2)}) copy-start(f32[72]{0:T(128)} %get-tuple-element.30) | copy-start | bytes 868
  38.3 5.2 %copy-start.36 = (f32[72]{0:T(128)S(1)}, f32[72]{0:T(128)}, u32[]{:S(2)}) copy-start(f32[72]{0:T(128)} %get-tuple-element.31) | copy-start | bytes 868
  43.5 3.7 %copy-start.13 = (bf16[48,16,8,72]{3,2,0,1:T(8,128)(2,1)S(1)}, bf16[48,16,8,72]{3,2,0,1:T(8,128)(2,1)}, u32[]{:S(2)}) copy-start(bf16[48,16,8,72]{3,2,0,1:T(8,128)(2,1)} %reshape.326) | copy-start | bytes 2654212
  45.6 15.3 %copy-start.26 = (f32[48,8,16]{2,1,0:T(8,128)}, f32[48,8,16]{2,1,0:T(8,128)S(1)}, u32[]{:S(2)}) copy-start(f32[48,8,16]{2,1,0:T(8,128)S(1)} %get-tuple-element.33) | copy-start | bytes 73732
  60.9 12.1 %copy-start.24 = (f32[48,16,8]{0,2,1:T(8,128)S(1)}, f32[48,16,8]{0,2,1:T(8,128)}, u32[]{:S(2)}) copy-start(f32[48,16,8]{0,2,1:T(8,128)} %get-tuple-element.23) | copy-start | bytes 73732
  60.9 12.3 %copy-start.25 = (f32[48,16,8]{0,2,1:T(8,128)S(1)}, f32[48,16,8]{0,2,1:T(8,128)}, u32[]{:S(2)}) copy-start(f32[48,16,8]{0,2,1:T(8,128)} %get-tuple-element.21) | copy-start | bytes 73732
  96.1 3.8 %copy-start.14 = (bf16[48,16,576]{2,1,0:T(8,128)(2,1)S(1)}, bf16[48,16,576]{2,1,0:T(8,128)(2,1)}, u32[]{:S(2)}) copy-start(bf16[48,16,576]{2,1,0:T(8,128)(2,1)} %reshape.330) | copy-start | bytes 2654212
  96.1 3.8 %copy-start.16 = (bf16[48,16,576]{2,1,0:T(8,128)(2,1)S(1)}, bf16[48,16,576]{2,1,0:T(8,128)(2,1)}, u32[]{:S(2)}) copy-start(bf16[48,16,576]{2,1,0:T(8,128)(2,1)} %reshape.329) | copy-start | bytes 2654212
  107.8 5.6 %copy-start.5 = (bf16[16,48,1152]{2,1,0:T(8,128)(2,1)S(1)}, bf16[16,48,1152]{2,1,0:T(8,128)(2,1)}, u32[]{:S(2)}) copy-start(bf16[16,48,1152]{2,1,0:T(8,128)(2,1)} %param.11) | copy-start | bytes 5308420
  119.2 46.9 %all-to-all-start.1 = ((bf16[16,48,1152]{2,1,0:T(8,128)(2,1)}), bf16[16,48,1152]{2,1,0:T(8,128)(2,1)}, u32[]{:S(2)}, u32[]{:S(2)}) async-start(bf16[16,48,1152]{2,1,0:T(8,128)(2,1)} %fusion.26), calls=%async_computation.1 | async-start | bytes 3538944 | tf_op jit(solution)/shard_map/all_to_all | solution.py:157
  128.0 3.9 %copy-start.29 = (f32[1152]{0:T(1024)S(1)}, f32[1152]{0:T(1024)}, u32[]{:S(2)}) copy-start(f32[1152]{0:T(1024)} %get-tuple-element.10) | copy-start | bytes 13828
  128.0 3.9 %copy-start.31 = (f32[1152]{0:T(1024)S(1)}, f32[1152]{0:T(1024)}, u32[]{:S(2)}) copy-start(f32[1152]{0:T(1024)} %get-tuple-element.14) | copy-start | bytes 13828
  138.7 29.2 %copy-start.30 = (f32[1152]{0:T(1024)S(1)}, f32[1152]{0:T(1024)}, u32[]{:S(2)}) copy-start(f32[1152]{0:T(1024)} %get-tuple-element.13) | copy-start | bytes 13828
  167.9 3.7 %copy-start.8 = (f32[8,2,48,1152]{3,2,0,1:T(8,128)}, f32[8,2,48,1152]{3,2,0,1:T(8,128)S(1)}, u32[]{:S(2)}) copy-start(f32[8,2,48,1152]{3,2,0,1:T(8,128)S(1)} %copy.214) | copy-start | bytes 10616836
  171.6 5.1 %copy-start.33 = (f32[72]{0:T(128)S(1)}, f32[72]{0:T(128)}, u32[]{:S(2)}) copy-start(f32[72]{0:T(128)} %get-tuple-element.29) | copy-start | bytes 868
  171.6 5.1 %copy-start.34 = (f32[72]{0:T(128)S(1)}, f32[72]{0:T(128)}, u32[]{:S(2)}) copy-start(f32[72]{0:T(128)} %get-tuple-element.32) | copy-start | bytes 868
  178.6 3.6 %copy-start.10 = (f32[2,8,384,384]{2,3,1,0:T(8,128)}, f32[2,8,384,384]{2,3,1,0:T(8,128)S(1)}, u32[]{:S(2)}) copy-start(f32[2,8,384,384]{2,3,1,0:T(8,128)S(1)} %get-tuple-element.41) | copy-start | bytes 28311556
  238.5 7.5 %copy-start.12 = (bf16[48,16,8,72]{3,2,0,1:T(8,128)(2,1)S(1)}, bf16[48,16,8,72]{3,2,0,1:T(8,128)(2,1)}, u32[]{:S(2)}) copy-start(bf16[48,16,8,72]{3,2,0,1:T(8,128)(2,1)} %reshape.355) | copy-start | bytes 2654212
  238.5 7.5 %copy-start.27 = (f32[48,8,16]{2,1,0:T(8,128)S(1)}, f32[48,8,16]{2,1,0:T(8,128)}, u32[]{:S(2)}) copy-start(f32[48,8,16]{2,1,0:T(8,128)} %copy-done.26) | copy-start | bytes 73732
  241.7 69.3 %all-to-all-start.2 = ((bf16[2,384,1152]{2,0,1:T(2,128)(2,1)}), bf16[2,384,1152]{2,0,1:T(2,128)(2,1)}, u32[]{:S(2)}, u32[]{:S(2)}) async-start(bf16[2,384,1152]{2,0,1:T(2,128)(2,1)} %copy.221), calls=%async_computation.2 | async-start | bytes 3538944 | tf_op jit(solution)/shard_map/all_to_all | solution.py:176
  255.3 5.6 %copy-start.9 = (f32[8,2,48,1152]{3,2,0,1:T(8,128)S(1)}, f32[8,2,48,1152]{3,2,0,1:T(8,128)}, u32[]{:S(2)}) copy-start(f32[8,2,48,1152]{3,2,0,1:T(8,128)} %copy-done.8) | copy-start | bytes 10616836
  255.3 5.6 %copy-start.42 = (bf16[576,1152]{1,0:T(8,128)(2,1)S(1)}, bf16[576,1152]{1,0:T(8,128)(2,1)}, u32[]{:S(2)}) copy-start(bf16[576,1152]{1,0:T(8,128)(2,1)} %param.16) | copy-start | bytes 3981316
  262.7 50.0 %copy-start.6 = (bf16[16,48,1152]{2,1,0:T(8,128)(2,1)S(1)}, bf16[16,48,1152]{2,1,0:T(8,128)(2,1)}, u32[]{:S(2)}) copy-start(bf16[16,48,1152]{2,1,0:T(8,128)(2,1)} %fusion.26) | copy-start | bytes 5308420
  (14 other events, 34.0 us)
where the time goes:
time: 321 us; the launch traced here: 315 us
  matrix products  113 us (35%)
  local copies, waits for them, and re-layouts  72.6 us (23%)
  blocking collectives  47.5 us (15%)
  other arithmetic  34.5 us (11%)
  waiting for transfers between devices  27.2 us (8%)
  starting transfers between devices  18.1 us (6%)
    psum x1, blocking collectives, body(): totals = lax.psum(term_stack, 'seq')  47.5 us
    dot_general x2, matrix products, attend(): jnp.einsum('bhlm,bmhd->blhd', score_grad, key_norm, preferred_element_typ...  30 us
    dot_general x2, matrix products, attend(): jnp.einsum('bhlm,blhd->bmhd', score_grad, query_norm, preferred_element_t...  29.3 us
    all_to_all x1, waiting for transfers between devices, body(): lax.all_to_all(mid_grad, 'seq', split_axis=0, concat_axis=1, tiled=True)  27.2 us
    dot_general x4, matrix products, matmul_back(): lax.dot_general(flattened, weight, (((1,), (1,)), ((), ())), preferred_el...  15.7 us
    unnamed x89, local copies, waits for them, and re-layouts  13.3 us
    dot_general x2, matrix products, attend(): jnp.einsum('blhd,bmhd->bhlm', cot_heads, value_heads, preferred_element_t...  10.3 us
    dot_general x3, matrix products, matmul_rows(): result = jnp.dot(flattened, weight, preferred_element_type=jnp.float32)  9.04 us
  transfers between devices with their start and end apart: 3, of which 1 were waited for; matrix products, arithmetic and copies ran while one was open for 43% of the time, Pallas kernels for 0%

commit v1 on v0

--- a/solution.py
+++ b/solution.py
@@ -154,7 +154,12 @@
     mid_grad = (out_grad.astype(jnp.float32) + temporal_branch).astype(jnp.bfloat16)
     arrived, landed = (
         lax.all_to_all(block_input, "seq", split_axis=0, concat_axis=1, tiled=True),
-        lax.all_to_all(mid_grad, "seq", split_axis=0, concat_axis=1, tiled=True),
+        jnp.concatenate(
+            lax.all_to_all(
+                jnp.stack(jnp.split(mid_grad, lax.axis_size("seq"), axis=0)), "seq", 0, 0
+            ),
+            axis=1,
+        ),
     )
     normed_fr, inverse_fr = layer_stats(arrived)
     frame_mod = modulate(normed_fr, modulation[0], modulation[1])

time: 321 us -> 341 us (1.062)
  local copies, waits for them, and re-layouts: 72.6 us -> 84.7 us
  other arithmetic: 34.5 us -> 41.7 us
    unnamed x89 -> x98, local copies, waits for them, and re-layouts: 13.3 us -> 18 us
  transfers between devices with their start and end apart: 3 -> 3, of which waited for: 1 -> 1; matrix products, arithmetic and copies ran while one was open for 43% -> 46% of each run, Pallas kernels for 0% -> 0%
where the time goes in v1:
time: 341 us; the launch traced here: 334 us
  matrix products  113 us (33%)
  local copies, waits for them, and re-layouts  84.7 us (25%)
  blocking collectives  47.5 us (14%)
  other arithmetic  41.7 us (12%)
  waiting for transfers between devices  27.2 us (8%)
  starting transfers between devices  18.1 us (5%)
    psum x1, blocking collectives, body(): totals = lax.psum(term_stack, 'seq')  47.5 us
    dot_general x2, matrix products, attend(): jnp.einsum('bhlm,bmhd->blhd', score_grad, key_norm, preferred_element_typ...  30.3 us
    dot_general x2, matrix products, attend(): jnp.einsum('bhlm,blhd->bmhd', score_grad, query_norm, preferred_element_t...  29.3 us
    all_to_all x1, waiting for transfers between devices, body(): lax.all_to_all(jnp.stack(jnp.split(mid_grad, lax.axis_size('seq'), axis=0...  27.2 us
    unnamed x98, local copies, waits for them, and re-layouts  18 us
    dot_general x4, matrix products, matmul_back(): lax.dot_general(flattened, weight, (((1,), (1,)), ((), ())), preferred_el...  15.7 us
    dot_general x2, matrix products, attend(): jnp.einsum('blhd,bmhd->bhlm', cot_heads, value_heads, preferred_element_t...  10.3 us
    convert_element_type x3, other arithmetic, rms_back(): return result.astype(jnp.bfloat16).reshape(values.shape[:-2] + (-1,))  9.97 us
  transfers between devices with their start and end apart: 3, of which 1 were waited for; matrix products, arithmetic and copies ran while one was open for 46% of the time, Pallas kernels for 0%

profile of v1, /device:TPU:0, one launch (start us, length us, event | category | flops | bytes accessed | tf_op | source)
XLA Modules:
  0.0 334.2 jit_solution(4211968290046407697)
XLA Ops:
  0.7 7.6 %all-to-all-start = ((bf16[16,48,1152]{2,1,0:T(8,128)(2,1)}), bf16[16,48,1152]{2,1,0:T(8,128)(2,1)}, u32[]{:S(2)}, u32[]{:S(2)}) async-start(bf16[16,48,1152]{2,1,0:T(8,128)(2,1)} %param.10), calls=%async_computation | async-start | bytes 3538944 | tf_op jit(solution)/shard_map/all_to_all | solution.py:156
  12.2 3.8 %reshape.326 = bf16[48,16,8,72]{3,2,0,1:T(8,128)(2,1)} reshape(bf16[48,16,576]{2,0,1:T(8,128)(2,1)} %fusion.98) | data formatting | bytes 1769472 | tf_op jit(solution)/shard_map/reshape | solution.py:39
  16.0 3.8 %convert_bitcast_fusion.2 = (f32[48,16,576]{2,0,1:T(8,128)S(1)}, bf16[48,16,576]{2,0,1:T(8,128)(2,1)}, f32[48,16,576]{2,0,1:T(8,128)}) fusion(bf16[3,16,48,576]{3,2,1,0:T(8,128)(2,1)} %param.12), kind=kLoop, calls=%fused_computation.89 | loop fusion | flops 884736 | bytes 7077888 | tf_op jit(solution)/shard_map/convert_element_type | solution.py:43
  34.4 2.9 multiply_reduce_fusion.6
  38.4 5.2 %fusion.94 = f32[48,8,16,16]{2,3,1,0:T(8,128)} fusion(bf16[48,16,8,72]{3,2,0,1:T(8,128)(2,1)S(1)} %copy-done.12, bf16[48,16,8,72]{3,2,0,1:T(8,128)(2,1)} %reshape.326), kind=kOutput, calls=%fused_computation.121 | convolution fusion | flops 14155776 | bytes 2162688 | tf_op jit(solution)/shard_map/blhd,bmhd->bhlm/dot_general | solution.py:72
  49.8 11.1 %fusion.38 = (f32[48,16,8]{1,2,0:T(8,128)}, f32[48,8,72,16]{2,3,1,0:T(8,128)}) fusion(f32[48,16,8,72]{3,2,1,0:T(8,128)} %reshape.338, f32[72]{0:T(128)S(1)} %copy-done.36, f32[48,8,16,16]{2,3,1,0:T(8,128)} %fusion.94, f32[48,8,16]{2,1,0:T(8,128)S(1)} %get-tuple-element.33, f32[48,8,16,16]{2,3,1,0:T(8,128)} %copy-done.18, f32[48,16,8,72]{3,2,1,0:T(8,128)} %reshape.337, ...), kind=kOutput, calls=%fused_computation.54 | convolution fusion | flops 17694736 | bytes 6169152 | tf_op jit(solution)/shard_map/bhlm,blhd->bmhd/dot_general | solution.py:83
  60.9 12.4 %fusion.41 = (f32[48,16,8]{1,2,0:T(8,128)}, f32[48,8,72,16]{2,3,1,0:T(8,128)}) fusion(f32[48,16,8,72]{3,2,1,0:T(8,128)} %reshape.337, f32[72]{0:T(128)S(1)} %copy-done.37, f32[48,8,16,16]{2,3,1,0:T(8,128)} %fusion.94, f32[48,8,16]{2,1,0:T(8,128)} %copy-done.24, f32[48,8,16,16]{2,3,1,0:T(8,128)} %copy-done.18, f32[48,16,8,72]{3,2,1,0:T(8,128)} %reshape.338, ...), kind=kOutput, calls=%fused_computation.59 | convolution fusion | flops 17694736 | bytes 6169152 | tf_op jit(solution)/shard_map/bhlm,bmhd->blhd/dot_general | solution.py:80
  77.9 3.0 copy.211
  80.9 3.7 %reshape.330 = bf16[48,16,576]{2,1,0:T(8,128)(2,1)} reshape(bf16[48,16,8,72]{3,2,1,0:T(8,128)(2,1)} %copy.211) | data formatting | bytes 1769472 | tf_op jit(solution)/shard_map/reshape | solution.py:91
  92.7 8.9 %fusion.37 = (bf16[48,16,8,72]{3,1,2,0:T(8,128)(2,1)S(1)}, bf16[48,16,8,72]{3,1,2,0:T(8,128)(2,1)}) fusion(f32[48,8,72,16]{2,3,1,0:T(8,128)} %get-tuple-element.38, f32[48,16,8,72]{3,2,1,0:T(8,128)} %reshape.338, f32[48,16,8]{1,2,0:T(8,128)} %copy.208, f32[48,16,8]{1,2,0:T(8,128)} %copy.204, f32[72]{0:T(128)} %get-tuple-element.30, ...), kind=kLoop, calls=%fused_computation.53 | loop fusion | flops 5308416 | bytes 8995392 | tf_op jit(solution)/shard_map/convert_element_type | solution.py:53
  103.2 3.7 %reshape.329 = bf16[48,16,576]{2,1,0:T(8,128)(2,1)} reshape(bf16[48,16,8,72]{3,2,1,0:T(8,128)(2,1)} %copy.209) | data formatting | bytes 1769472 | tf_op jit(solution)/shard_map/reshape | solution.py:53
  106.9 3.1 copy.203
  110.0 3.7 %reshape.328 = bf16[48,16,576]{2,1,0:T(8,128)(2,1)} reshape(bf16[48,16,8,72]{3,2,1,0:T(8,128)(2,1)} %copy.203) | data formatting | bytes 1769472 | tf_op jit(solution)/shard_map/reshape | solution.py:53
  113.6 5.6 %concatenate.13 = bf16[16,48,1728]{2,0,1:T(8,128)(2,1)} concatenate(bf16[16,48,576]{2,0,1:T(8,128)(2,1)} %bitcast.215, bf16[16,48,576]{2,0,1:T(8,128)(2,1)} %bitcast.214, bf16[16,48,576]{2,0,1:T(8,128)(2,1)} %bitcast.213), dimensions={2} | concatenate | bytes 5308416 | tf_op jit(solution)/shard_map/concatenate | solution.py:106
  122.2 5.5 %fusion.146 = (f32[1152]{0:T(1024)S(1)}, f32[768]{0:T(1024)S(1)}, f32[768,1152]{1,0:T(8,128)}) fusion(f32[1152]{0:T(1024)S(1)} %copy-done.29, bf16[768,1728]{1,0:T(8,128)(2,1)S(1)} %bitcast.222, bf16[1152,1728]{0,1:T(8,128)(2,1)S(1)} %copy-done.39), kind=kOutput, calls=%fused_computation.192 | convolution fusion | flops 3060300032 | bytes 10186752 | tf_op jit(solution)/shard_map/dot_general | solution.py:32
  127.8 3.3 fusion.23
  138.6 6.2 %all-to-all-start.1 = ((bf16[8,2,48,1152]{3,2,1,0:T(8,128)(2,1)}), bf16[8,2,48,1152]{3,2,1,0:T(8,128)(2,1)}, u32[]{:S(2)}, u32[]{:S(2)}) async-start(bf16[8,2,48,1152]{3,2,1,0:T(8,128)(2,1)} %fusion.116), calls=%async_computation.1 | async-start | bytes 3538944 | tf_op jit(solution)/shard_map/all_to_all | solution.py:158
  152.8 3.9 %fusion.33 = bf16[2,384,1728]{1,2,0:T(8,128)(2,1)S(1)} fusion(bf16[2,384,1152]{2,1,0:T(8,128)(2,1)S(1)} %add_convert_fusion, bf16[1152,1728]{0,1:T(8,128)(2,1)S(1)} %copy-done.40), kind=kOutput, calls=%fused_computation.48 | convolution fusion | flops 3058974720 | bytes 8404992 | tf_op jit(solution)/shard_map/dot_general | solution.py:26
  158.3 27.2 %all-to-all-done.1 = bf16[8,2,48,1152]{3,2,1,0:T(8,128)(2,1)} async-done(((bf16[8,2,48,1152]{3,2,1,0:T(8,128)(2,1)}), bf16[8,2,48,1152]{3,2,1,0:T(8,128)(2,1)}, u32[]{:S(2)}, u32[]{:S(2)}) %all-to-all-start.1) | async-done | bytes 1769504 | tf_op jit(solution)/shard_map/all_to_all | solution.py:158
  191.2 5.1 %fusion.156 = f32[2,8,384,384]{2,3,1,0:T(8,128)} fusion(bf16[2,384,8,72]{1,3,2,0:T(8,128)(2,1)S(1)} %bitcast.227, bf16[2,384,8,72]{1,3,2,0:T(8,128)(2,1)S(1)} %bitcast.220), kind=kOutput, calls=%fused_computation.195 | convolution fusion | flops 339738624 | bytes 11206656 | tf_op jit(solution)/shard_map/blhd,bmhd->bhlm/dot_general | solution.py:72
  198.3 3.6 %copy-done.11 = f32[2,8,384,384]{2,3,1,0:T(8,128)} copy-done((f32[2,8,384,384]{2,3,1,0:T(8,128)}, f32[2,8,384,384]{2,3,1,0:T(8,128)S(1)}, u32[]{:S(2)}) %copy-start.11) | copy-done | bytes 9437208
  201.9 3.0 fusion.105
  204.9 18.2 %fusion.63 = (f32[2,384,8]{1,2,0:T(8,128)S(1)}, f32[2,8,72,384]{3,2,1,0:T(8,128)}) fusion(bf16[2,384,8,72]{1,3,2,0:T(8,128)(2,1)S(1)} %bitcast.205, f32[72]{0:T(128)S(1)} %copy-done.34, f32[2,8,384,384]{2,3,1,0:T(8,128)} %fusion.156, f32[2,8,384]{2,1,0:T(8,128)S(1)} %get-tuple-element.40, f32[2,8,384,384]{2,3,1,0:T(8,128)} %copy-done.11, ...), kind=kOutput, calls=%fused_computation.96 | convolution fusion | flops 364511616 | bytes 22487616 | tf_op jit(solution)/shard_map/bhlm,blhd->bmhd/dot_general | solution.py:83
  223.1 17.9 %fusion.70 = (f32[2,384,8]{1,2,0:T(8,128)S(1)}, f32[2,8,72,384]{3,2,1,0:T(8,128)}) fusion(bf16[2,384,8,72]{1,3,2,0:T(8,128)(2,1)S(1)} %bitcast.211, f32[72]{0:T(128)S(1)} %copy-done.35, f32[2,8,384,384]{2,3,1,0:T(8,128)} %fusion.156, f32[2,8,384]{2,1,0:T(8,128)S(1)} %get-tuple-element.40, f32[2,8,384,384]{2,3,1,0:T(8,128)} %copy-done.11, ...), kind=kOutput, calls=%fused_computation.103 | convolution fusion | flops 364511616 | bytes 22487616 | tf_op jit(solution)/shard_map/bhlm,bmhd->blhd/dot_general | solution.py:80
  248.0 6.2 %multiply_reduce_fusion.1 = (f32[1152]{0:T(1024)S(1)}, f32[768]{0:T(1024)S(1)}, f32[768]{0:T(1024)S(1)}, f32[1152]{0:T(1024)S(1)}, f32[768,1152]{1,0:T(8,128)}) fusion(f32[8,2,48,1152]{3,2,0,1:T(8,128)S(1)} %copy-done.4, f32[768]{0:T(1024)S(1)} %rsqrt.74, f32[768]{0:T(1024)S(1)} %div.96, f32[1152]{0:T(1024)S(1)} %copy-done.30, ...), kind=kOutput, calls=%fused_computation.43 | convolution fusion | flops 3073569280 | bytes 13739520 | tf_op jit(solution)/shard_map/dot_general | solution.py:32
  254.2 3.9 %multiply_convert_fusion.1 = bf16[2,384,1152]{2,1,0:T(8,128)(2,1)S(1)} fusion(f32[2,384,1152]{2,1,0:T(8,128)} %bitcast.219, f32[8,2,48,1152]{3,2,0,1:T(8,128)} %copy-done.3, f32[2,384]{1,0:T(2,128)S(1)} %div.98, f32[2,384]{1,0:T(2,128)S(1)} %div.95, f32[1152]{0:T(1024)S(1)} %copy-done.30, f32[2,384]{1,0:T(2,128)S(1)} %div.87, f32[2,384]{1,0:T(2,128)S(1)} %rsqrt.71), kind=kLoop, calls=%fused_computation.44 | loop fusion | flops 7077888 | bytes 8864256 | tf_op jit(solution)/shard_map/convert_element_type | solution.py:180
  258.1 3.0 copy.221
  261.1 4.3 %all-to-all-start.2 = ((bf16[2,384,1152]{2,0,1:T(2,128)(2,1)}), bf16[2,384,1152]{2,0,1:T(2,128)(2,1)}, u32[]{:S(2)}, u32[]{:S(2)}) async-start(bf16[2,384,1152]{2,0,1:T(2,128)(2,1)} %copy.221), calls=%async_computation.2 | async-start | bytes 3538944 | tf_op jit(solution)/shard_map/all_to_all | solution.py:181
  265.5 3.4 %fusion.83 = bf16[48,16,8,72]{3,1,2,0:T(8,128)(2,1)S(1)} fusion(bf16[48,16,8,72]{3,2,0,1:T(8,128)(2,1)S(1)} %copy-done.13, f32[48,8,16,16]{2,3,1,0:T(8,128)} %copy-done.18, f32[48,8,16]{2,1,0:T(8,128)S(1)} %copy-done.25), kind=kOutput, calls=%fused_computation.115 | convolution fusion | flops 14893056 | bytes 2187264 | tf_op jit(solution)/shard_map/bhlm,bmhd->blhd/dot_general | solution.py:69
  271.3 3.5 %fusion.81 = f32[1152]{0:T(1024)S(1)} fusion(bf16[16,48,1152]{2,1,0:T(8,128)(2,1)} %param.13, bf16[576,1152]{1,0:T(8,128)(2,1)S(1)} %copy-done, bf16[16,48,576]{2,0,1:T(8,128)(2,1)} %bitcast.223), kind=kOutput, calls=%fused_computation.113 | convolution fusion | flops 1021868928 | bytes 3985920 | tf_op jit(solution)/shard_map/dot_general | solution.py:26
  274.9 5.6 %fusion.90 = bf16[2,8,72,384]{3,2,1,0:T(8,128)(2,1)S(1)} fusion(bf16[2,384,8,72]{1,3,2,0:T(8,128)(2,1)S(1)} %bitcast.221, f32[2,8,384,384]{2,3,1,0:T(8,128)} %copy-done.11, f32[2,8,384]{2,1,0:T(8,128)S(1)} %get-tuple-element.40), kind=kOutput, calls=%fused_computation.118 | convolution fusion | flops 347258880 | bytes 11231232 | tf_op jit(solution)/shard_map/bhlm,bmhd->blhd/dot_general | solution.py:69
  282.3 47.5 %psum.7 = f32[6,1152]{1,0:T(8,128)S(1)} all-reduce(f32[6,1152]{1,0:T(8,128)S(1)} %stack.63), channel_id=1, replica_groups=mesh['clip'=4,'seq'=8] {'seq'}, use_global_device_ids=true, to_apply=%region_26.0 | all-reduce | flops 6912 | bytes 55296 | tf_op jit(solution)/shard_map/psum | solution.py:192
  (179 shorter events, 82.7 us)
Async XLA Ops:
  0.6 8.9 %copy-start = (bf16[576,1152]{1,0:T(8,128)(2,1)S(1)}, bf16[576,1152]{1,0:T(8,128)(2,1)}, u32[]{:S(2)}) copy-start(bf16[576,1152]{1,0:T(8,128)(2,1)} %param.18) | copy-start | bytes 3981316
  0.6 7.6 %copy-start.38 = (f32[4,72]{1,0:T(4,128)S(1)}, f32[4,72]{1,0:T(4,128)}, u32[]{:S(2)}) copy-start(f32[4,72]{1,0:T(4,128)} %param.19) | copy-start | bytes 3460
  0.7 8.2 %copy-start.33 = (f32[5,1152]{1,0:T(8,128)S(1)}, f32[5,1152]{1,0:T(8,128)}, u32[]{:S(2)}) copy-start(f32[5,1152]{1,0:T(8,128)} %param.14) | copy-start | bytes 69124
  0.7 8.8 %copy-start.19 = (bf16[16,48,1152]{2,1,0:T(8,128)(2,1)S(1)}, bf16[16,48,1152]{2,1,0:T(8,128)(2,1)}, u32[]{:S(2)}) copy-start(bf16[16,48,1152]{2,1,0:T(8,128)(2,1)} %param.13) | copy-start | bytes 5308420
  0.7 137.9 %all-to-all-start = ((bf16[16,48,1152]{2,1,0:T(8,128)(2,1)}), bf16[16,48,1152]{2,1,0:T(8,128)(2,1)}, u32[]{:S(2)}, u32[]{:S(2)}) async-start(bf16[16,48,1152]{2,1,0:T(8,128)(2,1)} %param.10), calls=%async_computation | async-start | bytes 3538944 | tf_op jit(solution)/shard_map/all_to_all | solution.py:156
  23.0 3.9 %copy-start.15 = (bf16[48,16,576]{2,0,1:T(8,128)(2,1)S(1)}, bf16[48,16,576]{2,0,1:T(8,128)(2,1)}, u32[]{:S(2)}) copy-start(bf16[48,16,576]{2,0,1:T(8,128)(2,1)} %get-tuple-element.16) | copy-start | bytes 2654212
  34.4 3.9 %copy-start.12 = (bf16[48,16,8,72]{3,2,0,1:T(8,128)(2,1)S(1)}, bf16[48,16,8,72]{3,2,0,1:T(8,128)(2,1)}, u32[]{:S(2)}) copy-start(bf16[48,16,8,72]{3,2,0,1:T(8,128)(2,1)} %reshape.354) | copy-start | bytes 2654212
  38.3 5.2 %copy-start.1 = (f32[48,16,8,72]{3,2,1,0:T(8,128)S(1)}, f32[48,16,8,72]{3,2,1,0:T(8,128)}, u32[]{:S(2)}) copy-start(f32[48,16,8,72]{3,2,1,0:T(8,128)} %reshape.337) | copy-start | bytes 5308420
  38.3 5.2 %copy-start.2 = (f32[48,16,8,72]{3,2,1,0:T(8,128)S(1)}, f32[48,16,8,72]{3,2,1,0:T(8,128)}, u32[]{:S(2)}) copy-start(f32[48,16,8,72]{3,2,1,0:T(8,128)} %reshape.338) | copy-start | bytes 5308420
  38.3 5.2 %copy-start.36 = (f32[72]{0:T(128)S(1)}, f32[72]{0:T(128)}, u32[]{:S(2)}) copy-start(f32[72]{0:T(128)} %get-tuple-element.30) | copy-start | bytes 868
  38.4 5.2 %copy-start.37 = (f32[72]{0:T(128)S(1)}, f32[72]{0:T(128)}, u32[]{:S(2)}) copy-start(f32[72]{0:T(128)} %get-tuple-element.31) | copy-start | bytes 868
  43.6 3.7 %copy-start.14 = (bf16[48,16,8,72]{3,2,0,1:T(8,128)(2,1)S(1)}, bf16[48,16,8,72]{3,2,0,1:T(8,128)(2,1)}, u32[]{:S(2)}) copy-start(bf16[48,16,8,72]{3,2,0,1:T(8,128)(2,1)} %reshape.326) | copy-start | bytes 2654212
  45.6 4.2 %copy-start.24 = (f32[48,8,16]{2,1,0:T(8,128)}, f32[48,8,16]{2,1,0:T(8,128)S(1)}, u32[]{:S(2)}) copy-start(f32[48,8,16]{2,1,0:T(8,128)S(1)} %get-tuple-element.33) | copy-start | bytes 73732
  60.9 12.4 %copy-start.5 = (bf16[16,48,1152]{2,1,0:T(8,128)(2,1)S(1)}, bf16[16,48,1152]{2,1,0:T(8,128)(2,1)}, u32[]{:S(2)}) copy-start(bf16[16,48,1152]{2,1,0:T(8,128)(2,1)} %param.11) | copy-start | bytes 5308420
  122.2 5.6 %copy-start.27 = (f32[16,48]{1,0:T(8,128)S(1)}, f32[16,48]{1,0:T(8,128)}, u32[]{:S(2)}) copy-start(f32[16,48]{1,0:T(8,128)} %copy-done.26) | copy-start | bytes 9220
  122.2 5.6 %copy-start.28 = (f32[16,48]{1,0:T(8,128)S(1)}, f32[16,48]{1,0:T(8,128)}, u32[]{:S(2)}) copy-start(f32[16,48]{1,0:T(8,128)} %add_rsqrt_fusion.5) | copy-start | bytes 9220
  127.8 3.6 %copy-start.20 = (bf16[16,48,1152]{2,1,0:T(8,128)(2,1)S(1)}, bf16[16,48,1152]{2,1,0:T(8,128)(2,1)}, u32[]{:S(2)}) copy-start(bf16[16,48,1152]{2,1,0:T(8,128)(2,1)} %param.13) | copy-start | bytes 5308420
  132.9 5.0 %copy-start.6 = (bf16[16,48,1152]{2,1,0:T(8,128)(2,1)}, bf16[16,48,1152]{2,1,0:T(8,128)(2,1)S(1)}, u32[]{:S(2)}) copy-start(bf16[16,48,1152]{2,1,0:T(8,128)(2,1)S(1)} %fusion.26) | copy-start | bytes 5308420
  138.6 46.9 %all-to-all-start.1 = ((bf16[8,2,48,1152]{3,2,1,0:T(8,128)(2,1)}), bf16[8,2,48,1152]{3,2,1,0:T(8,128)(2,1)}, u32[]{:S(2)}, u32[]{:S(2)}) async-start(bf16[8,2,48,1152]{3,2,1,0:T(8,128)(2,1)} %fusion.116), calls=%async_computation.1 | async-start | bytes 3538944 | tf_op jit(solution)/shard_map/all_to_all | solution.py:158
  147.3 3.9 %copy-start.30 = (f32[1152]{0:T(1024)S(1)}, f32[1152]{0:T(1024)}, u32[]{:S(2)}) copy-start(f32[1152]{0:T(1024)} %get-tuple-element.10) | copy-start | bytes 13828
  147.3 3.9 %copy-start.32 = (f32[1152]{0:T(1024)S(1)}, f32[1152]{0:T(1024)}, u32[]{:S(2)}) copy-start(f32[1152]{0:T(1024)} %get-tuple-element.14) | copy-start | bytes 13828
  187.5 3.7 %copy-start.9 = (f32[2,8,48,1152]{3,2,1,0:T(8,128)}, f32[2,8,48,1152]{3,2,1,0:T(8,128)S(1)}, u32[]{:S(2)}) copy-start(f32[2,8,48,1152]{3,2,1,0:T(8,128)S(1)} %copy.214) | copy-start | bytes 10616836
  191.2 5.1 %copy-start.34 = (f32[72]{0:T(128)S(1)}, f32[72]{0:T(128)}, u32[]{:S(2)}) copy-start(f32[72]{0:T(128)} %get-tuple-element.29) | copy-start | bytes 868
  191.2 5.1 %copy-start.35 = (f32[72]{0:T(128)S(1)}, f32[72]{0:T(128)}, u32[]{:S(2)}) copy-start(f32[72]{0:T(128)} %get-tuple-element.32) | copy-start | bytes 868
  198.3 3.6 %copy-start.11 = (f32[2,8,384,384]{2,3,1,0:T(8,128)}, f32[2,8,384,384]{2,3,1,0:T(8,128)S(1)}, u32[]{:S(2)}) copy-start(f32[2,8,384,384]{2,3,1,0:T(8,128)S(1)} %get-tuple-element.41) | copy-start | bytes 28311556
  258.1 7.4 %copy-start.13 = (bf16[48,16,8,72]{3,2,0,1:T(8,128)(2,1)S(1)}, bf16[48,16,8,72]{3,2,0,1:T(8,128)(2,1)}, u32[]{:S(2)}) copy-start(bf16[48,16,8,72]{3,2,0,1:T(8,128)(2,1)} %reshape.354) | copy-start | bytes 2654212
  258.1 7.4 %copy-start.25 = (f32[48,8,16]{2,1,0:T(8,128)S(1)}, f32[48,8,16]{2,1,0:T(8,128)}, u32[]{:S(2)}) copy-start(f32[48,8,16]{2,1,0:T(8,128)} %copy-done.24) | copy-start | bytes 73732
  261.1 69.3 %all-to-all-start.2 = ((bf16[2,384,1152]{2,0,1:T(2,128)(2,1)}), bf16[2,384,1152]{2,0,1:T(2,128)(2,1)}, u32[]{:S(2)}, u32[]{:S(2)}) async-start(bf16[2,384,1152]{2,0,1:T(2,128)(2,1)} %copy.221), calls=%async_computation.2 | async-start | bytes 3538944 | tf_op jit(solution)/shard_map/all_to_all | solution.py:181
  271.3 3.5 %copy-start.17 = (bf16[2,384,576]{1,2,0:T(8,128)(2,1)S(1)}, bf16[2,384,576]{1,2,0:T(8,128)(2,1)}, u32[]{:S(2)}) copy-start(bf16[2,384,576]{1,2,0:T(8,128)(2,1)} %get-tuple-element.18) | copy-start | bytes 2654212
  274.8 5.6 %copy-start.10 = (f32[2,8,48,1152]{3,2,1,0:T(8,128)S(1)}, f32[2,8,48,1152]{3,2,1,0:T(8,128)}, u32[]{:S(2)}) copy-start(f32[2,8,48,1152]{3,2,1,0:T(8,128)} %copy-done.9) | copy-start | bytes 10616836
  274.8 5.6 %copy-start.43 = (bf16[576,1152]{1,0:T(8,128)(2,1)S(1)}, bf16[576,1152]{1,0:T(8,128)(2,1)}, u32[]{:S(2)}) copy-start(bf16[576,1152]{1,0:T(8,128)(2,1)} %param.16) | copy-start | bytes 3981316
  282.2 50.0 %copy-start.7 = (bf16[16,48,1152]{2,1,0:T(8,128)(2,1)S(1)}, bf16[16,48,1152]{2,1,0:T(8,128)(2,1)}, u32[]{:S(2)}) copy-start(bf16[16,48,1152]{2,1,0:T(8,128)(2,1)} %copy-done.6) | copy-start | bytes 5308420
  (15 other events, 32.2 us)
